TPU v7x, 512 devices: a whole 4x8x8 slice. The times are simulated.
512 devices in a mesh: dp: 32 (over x, y), tensor: 16 (over z, core).
Axes of the slice: x: 4, y: 8, z: 8, core: 2. Of those that a mesh axis runs over, the one named last changes fastest.
Arguments:
- queries: bfloat16 [4096, 16384], P('dp', 'tensor'), may hold values from -24 to 24
- draft_keys: bfloat16 [4096, 1024], P('dp'), may hold values from -6 to 6
- draft_values: bfloat16 [4096, 1024], P('dp'), may hold values from -6 to 6
- cache_keys: bfloat16 [64, 2048, 1024], P('dp', 'tensor'), may hold values from -24 to 24
- cache_values: bfloat16 [64, 2048, 1024], P('dp', 'tensor'), may hold values from -6 to 6
- out_weight: bfloat16 [16384, 16384], P('tensor', 'dp'), may hold values from -0.25 to 0.25
- cache_lengths: int32 [64], P('dp'), may hold values from 512 to 2048
- draft_lengths: int32 [64], replicated, may hold values from 8 to 64
- dest_group: int32 [64], replicated, may hold values from 0 to 31, as said below
- dest_offset: int32 [64], replicated, may hold values from 0 to 32, as said below
Outputs:
- verified: bfloat16 [3072, 16384], P('tensor', 'dp')
Inputs may be any that keep to these rules, and one draw needn't show every extreme that they name: `dest_group`: at most one request of a group has another group as destination, and each group receives at most one such request. `dest_offset`: blocks with the same destination never intersect and end at packed row 96 or before; a block moved to another group starts right after that group's own rows; in every draw some group's blocks fill all 96 rows.
All inputs are finite; a program needn't handle non-finite values.
Results may differ from a plain program's by a relative error of at most 0.017.
Values may be sent and summed in bfloat16 or wider, within the bound.
No kernel may reach another device: no remote copies, remote signals or barrier semaphores. Data moves between devices by JAX's collectives and lax.ppermute only.
A program may use at most 64 MiB of HBM per device.

v0:
```python
import jax
import jax.numpy as jnp
from jax import lax
from jax.sharding import PartitionSpec as P

HEADS = 128
KV_HEADS = 8
HEAD_DIM = 128
DRAFT = 64
GROUP_REQ = 2
PACK = 96
NEG_FILL = -1e30


def packed_sources(row_ids, draft_lengths, dest_group, dest_offset):
    request_ids = jnp.arange(dest_group.shape[0], dtype=jnp.int32)
    slot_group = row_ids // PACK
    slot_index = row_ids % PACK
    inside = (
        (dest_group[None, :] == slot_group[:, None])
        & (slot_index[:, None] >= dest_offset[None, :])
        & (slot_index[:, None] < (dest_offset + draft_lengths)[None, :])
    )
    request = jnp.sum(jnp.where(inside, request_ids[None, :], 0), axis=1)
    first_slot = jnp.sum(jnp.where(inside, dest_offset[None, :], 0), axis=1)
    return (request, slot_index - first_slot, jnp.any(inside, axis=1))


def attend_one(operands):
    queries_one, cache_k, cache_v, draft_k, draft_v, cache_len, draft_len = operands
    score_scale = HEAD_DIM ** (-0.5)
    cache_scores = (
        jnp.einsum("qkgd,lkd->kgql", queries_one, cache_k, preferred_element_type=jnp.float32)
        * score_scale
    )
    draft_scores = (
        jnp.einsum("qkgd,jkd->kgqj", queries_one, draft_k, preferred_element_type=jnp.float32)
        * score_scale
    )
    cache_pos = jnp.arange(cache_k.shape[0], dtype=jnp.int32)
    draft_pos = jnp.arange(draft_k.shape[0], dtype=jnp.int32)
    keep_cache = cache_pos < cache_len
    keep_draft = (draft_pos[None, :] <= draft_pos[:, None]) & (draft_pos[None, :] < draft_len)
    cache_scores = jnp.where(keep_cache, cache_scores, NEG_FILL)
    draft_scores = jnp.where(keep_draft, draft_scores, NEG_FILL)
    highest = jnp.maximum(
        jnp.max(cache_scores, axis=-1, keepdims=True), jnp.max(draft_scores, axis=-1, keepdims=True)
    )
    cache_exp = jnp.exp(cache_scores - highest)
    draft_exp = jnp.exp(draft_scores - highest)
    denominator = jnp.sum(cache_exp, axis=-1, keepdims=True) + jnp.sum(
        draft_exp, axis=-1, keepdims=True
    )
    cache_weights = (cache_exp / denominator).astype(jnp.bfloat16)
    draft_weights = (draft_exp / denominator).astype(jnp.bfloat16)
    mixed = jnp.einsum("kgql,lkd->qkgd", cache_weights, cache_v, preferred_element_type=jnp.float32)
    mixed = mixed + jnp.einsum(
        "kgqj,jkd->qkgd", draft_weights, draft_v, preferred_element_type=jnp.float32
    )
    is_live = draft_pos < draft_len
    return jnp.where(is_live[:, None, None, None], mixed, 0.0).astype(jnp.bfloat16)


def body(
    queries,
    draft_keys,
    draft_values,
    cache_keys,
    cache_values,
    out_weight,
    cache_lengths,
    draft_lengths,
    dest_group,
    dest_offset,
):
    tensor_count = lax.axis_size("tensor")
    data_count = lax.axis_size("dp")
    my_rank = lax.axis_index("tensor")
    my_group = lax.axis_index("dp")
    local_heads = HEADS // tensor_count
    group_heads = HEADS // KV_HEADS
    kv_local = max(1, local_heads // group_heads)
    per_kv = local_heads // kv_local
    kv_width = kv_local * HEAD_DIM
    span_rows = cache_keys.shape[1]
    copies = tensor_count // KV_HEADS

    def spread(cache_block):
        return jnp.repeat(
            cache_block.reshape(GROUP_REQ, span_rows, KV_HEADS, HEAD_DIM), copies, axis=2
        )

    full_keys, full_values = (
        lax.all_to_all(spread(cache_keys), "tensor", split_axis=2, concat_axis=1, tiled=True),
        lax.all_to_all(spread(cache_values), "tensor", split_axis=2, concat_axis=1, tiled=True),
    )
    kv_first = my_rank * local_heads // group_heads
    draft_k = lax.dynamic_slice_in_dim(draft_keys, kv_first * HEAD_DIM, kv_width, 1).reshape(
        GROUP_REQ, DRAFT, kv_local, HEAD_DIM
    )
    draft_v = lax.dynamic_slice_in_dim(draft_values, kv_first * HEAD_DIM, kv_width, 1).reshape(
        GROUP_REQ, DRAFT, kv_local, HEAD_DIM
    )
    local_queries = queries.reshape(GROUP_REQ, DRAFT, kv_local, per_kv, HEAD_DIM)
    my_lengths = lax.dynamic_slice_in_dim(draft_lengths, my_group * GROUP_REQ, GROUP_REQ)
    attended = lax.map(
        attend_one,
        (local_queries, full_keys, full_values, draft_k, draft_v, cache_lengths, my_lengths),
    )
    width_local = local_heads * HEAD_DIM
    attended_rows = attended.reshape(GROUP_REQ * DRAFT, width_local)
    target_rows = PACK * data_count // tensor_count
    home_all = lax.all_gather(attended_rows, "dp", axis=0, tiled=True)
    row_ids = jnp.arange(lax.axis_size("tensor") * target_rows, dtype=jnp.int32)
    request, within, is_live = packed_sources(row_ids, draft_lengths, dest_group, dest_offset)
    picked = jnp.take(home_all, request * DRAFT + within, axis=0)
    picked = jnp.where(is_live[:, None], picked, jnp.zeros((), jnp.bfloat16))
    return lax.psum_scatter(
        jnp.dot(picked, out_weight, preferred_element_type=jnp.float32).astype(jnp.bfloat16),
        "tensor",
        scatter_dimension=0,
        tiled=True,
    )


def solution(mesh):
    in_specs = (
        P("dp", "tensor"),
        P("dp", None),
        P("dp", None),
        P("dp", "tensor", None),
        P("dp", "tensor", None),
        P("tensor", "dp"),
        P("dp"),
        P(),
        P(),
        P(),
    )
    out_specs = P("tensor", "dp")
    return jax.shard_map(body, mesh=mesh, in_specs=in_specs, out_specs=out_specs, check_vma=False)
```

profile of v0, /device:TPU:8, one launch (start us, length us, event | category | flops | bytes accessed | tf_op | source)
XLA Modules:
  0.0 296.0 jit_solution(7023909836648568548)
XLA Ops:
  6.5 1.3 copy_bitcast_fusion.3
  7.9 1.2 broadcast_in_dim.102
  9.1 10.4 %all-to-all-start.1 = ((bf16[2,128,16,128]{3,1,0,2:T(8,128)(2,1)}), bf16[2,128,16,128]{3,1,0,2:T(8,128)(2,1)S(1)}, u32[]{:S(2)}, u32[]{:S(2)}) async-start(bf16[2,128,16,128]{3,1,0,2:T(8,128)(2,1)} %bitcast.25), calls=%async_computation.1 | async-start | bytes 2097152 | tf_op jit(solution)/shard_map/all_to_all | solution.py:94
  19.7 26.3 %all-to-all-done.1 = bf16[2,128,16,128]{3,1,0,2:T(8,128)(2,1)S(1)} async-done(((bf16[2,128,16,128]{3,1,0,2:T(8,128)(2,1)}), bf16[2,128,16,128]{3,1,0,2:T(8,128)(2,1)S(1)}, u32[]{:S(2)}, u32[]{:S(2)}) %all-to-all-start.1) | async-done | bytes 1048608 | tf_op jit(solution)/shard_map/all_to_all | solution.py:94
  46.0 1.3 broadcast_in_dim.101
  47.3 5.0 %all-to-all-start = ((bf16[2,128,16,128]{3,1,0,2:T(8,128)(2,1)}), bf16[2,128,16,128]{3,1,0,2:T(8,128)(2,1)}, u32[]{:S(2)}, u32[]{:S(2)}) async-start(bf16[2,128,16,128]{3,1,0,2:T(8,128)(2,1)} %bitcast.20), calls=%async_computation | async-start | bytes 2097152 | tf_op jit(solution)/shard_map/all_to_all | solution.py:95
  52.5 0.8 constant_dynamic-slice_fusion.1
  53.4 25.4 %all-to-all-done = bf16[2,128,16,128]{3,1,0,2:T(8,128)(2,1)} async-done(((bf16[2,128,16,128]{3,1,0,2:T(8,128)(2,1)}), bf16[2,128,16,128]{3,1,0,2:T(8,128)(2,1)}, u32[]{:S(2)}, u32[]{:S(2)}) %all-to-all-start) | async-done | bytes 1048608 | tf_op jit(solution)/shard_map/all_to_all | solution.py:95
  78.8 1.3 copy.36
  80.1 14.2 %while.10 = (s32[]{:T(128)}, bf16[2,64,1,8,128]{4,3,1,0,2:T(8,128)(2,1)}, s32[2]{0:T(128)S(1)}, bf16[2,2048,1,128]{3,1,2,0:T(8,128)(2,1)S(1)}, s32[2]{0:T(128)S(...) while((s32[]{:T(128)}, ...), condition=%wide.region_8.9_spmd, body=%wide.region_3.8_spmd.sunk | while | flops 566699072 | bytes 15692581 | solution.py:106
  80.1 0.7 dynamic_slice.73
  80.8 0.7 iota_compare_fusion.6
  81.5 0.7 dynamic_slice.72
  82.2 0.7 iota_compare_fusion.5
  83.2 0.9 bitcast_reduce_fusion.2
  84.2 0.9 fusion.71
  85.1 1.1 fusion.73
  86.5 0.7 copy_dynamic-update-slice_fusion.2
  87.2 0.7 dynamic_slice.73
  87.9 0.7 iota_compare_fusion.6
  88.6 0.7 dynamic_slice.72
  89.3 0.7 iota_compare_fusion.5
  90.3 0.9 bitcast_reduce_fusion.2
  91.3 0.9 fusion.71
  92.2 1.1 fusion.73
  93.6 0.7 copy_dynamic-update-slice_fusion.2
  94.3 1.7 copy.62
  96.1 0.4 fusion.50
  97.0 99.9 %all-gather.2.cloned.1.call-done = bf16[4096,1024]{1,0:T(8,128)(2,1)} async-done(((bf16[128,1024]{1,0:T(8,128)(2,1)}), bf16[4096,1024]{1,0:T(8,128)(2,1)}) %all-gather.2.cloned.1.call-update) | async-done | bytes 8388624 | tf_op jit(solution)/shard_map/all_gather | solution.py:113
  196.9 20.4 %gather_fusion = bf16[3072,1024]{1,0:T(8,128)(2,1)} fusion(bf16[4096,1024]{1,0:T(8,128)(2,1)} %all-gather.2.cloned.1.call-done, s32[3072]{0:T(1024)S(1)} %broadcast_clamp_fusion), kind=kCustom, calls=%fused_computation | custom fusion | bytes 12595200 | tf_op jit(solution)/shard_map/jit(_take)/gather | solution.py:116
  217.3 7.6 %fusion.34 = bf16[3072,512]{1,0:T(8,128)(2,1)} fusion(bf16[1024,512]{1,0:T(8,128)(2,1)S(1)} %copy-done, bf16[3072,1024]{1,0:T(8,128)(2,1)} %gather_fusion, pred[3072]{0:T(1024)(128)(4,1)S(1)} %compare_and_fusion.1, pred[3072]{0:T(1024)(128)(4,1)S(1)} %fusion.50), kind=kOutput, calls=%fused_computation.49 | convolution fusion | flops 3229089792 | bytes 10491904 | tf_op jit(solution)/shard_map/dot_general | solution.py:119
  224.9 64.2 %reduce-scatter.2.cloned.1.call-done = bf16[192,512]{1,0:T(8,128)(2,1)} async-done(((bf16[3072,512]{1,0:T(8,128)(2,1)}), bf16[192,512]{1,0:T(8,128)(2,1)}) %reduce-scatter.2.cloned.1.call-update) | async-done | bytes 196624 | tf_op jit(solution)/shard_map/reduce_scatter | solution.py:118
  (44 shorter events, 2.3 us)
Async XLA Ops:
  6.5 210.7 %copy-start = (bf16[1024,512]{1,0:T(8,128)(2,1)S(1)}, bf16[1024,512]{1,0:T(8,128)(2,1)}, u32[]{:S(2)}) copy-start(bf16[1024,512]{1,0:T(8,128)(2,1)} %param.17) | copy-start | bytes 3145732
  6.5 13.0 %copy-start.1 = (bf16[2,128,1024]{2,1,0:T(8,128)(2,1)S(1)}, bf16[2,128,1024]{2,1,0:T(8,128)(2,1)}, u32[]{:S(2)}) copy-start(bf16[2,128,1024]{2,1,0:T(8,128)(2,1)} %param.16) | copy-start | bytes 1572868
  7.8 44.5 %copy-start.2 = (bf16[128,1024]{1,0:T(8,128)(2,1)S(1)}, bf16[128,1024]{1,0:T(8,128)(2,1)}, u32[]{:S(2)}) copy-start(bf16[128,1024]{1,0:T(8,128)(2,1)} %param.12) | copy-start | bytes 786436
  7.8 44.6 %copy-start.6 = (s32[64]{0:T(128)S(1)}, s32[64]{0:T(128)}, u32[]{:S(2)}) copy-start(s32[64]{0:T(128)} %param.19) | copy-start | bytes 772
  9.1 36.9 %all-to-all-start.1 = ((bf16[2,128,16,128]{3,1,0,2:T(8,128)(2,1)}), bf16[2,128,16,128]{3,1,0,2:T(8,128)(2,1)S(1)}, u32[]{:S(2)}, u32[]{:S(2)}) async-start(bf16[2,128,16,128]{3,1,0,2:T(8,128)(2,1)} %bitcast.25), calls=%async_computation.1 | async-start | bytes 2097152 | tf_op jit(solution)/shard_map/all_to_all | solution.py:94
  19.7 60.4 %copy-start.5 = (s32[2]{0:T(128)S(1)}, s32[2]{0:T(128)}, u32[]{:S(2)}) copy-start(s32[2]{0:T(128)} %param.18) | copy-start | bytes 28
  47.3 31.5 %all-to-all-start = ((bf16[2,128,16,128]{3,1,0,2:T(8,128)(2,1)}), bf16[2,128,16,128]{3,1,0,2:T(8,128)(2,1)}, u32[]{:S(2)}, u32[]{:S(2)}) async-start(bf16[2,128,16,128]{3,1,0,2:T(8,128)(2,1)} %bitcast.20), calls=%async_computation | async-start | bytes 2097152 | tf_op jit(solution)/shard_map/all_to_all | solution.py:95
  52.3 144.6 %all-gather.2.cloned.1.call-start = ((), (), s32[]{:S(2)}) async-start(), calls=%async_computation.3 | async-start | bytes 8650752 | tf_op jit(solution)/shard_map/all_gather | solution.py:113
  80.1 16.0 %copy-start.3 = (s32[64]{0:T(128)S(1)}, s32[64]{0:T(128)}, u32[]{:S(2)}) copy-start(s32[64]{0:T(128)} %param.21) | copy-start | bytes 772
  80.1 16.0 %copy-start.4 = (s32[64]{0:T(128)S(1)}, s32[64]{0:T(128)}, u32[]{:S(2)}) copy-start(s32[64]{0:T(128)} %param.20) | copy-start | bytes 772
  96.0 193.2 %reduce-scatter.2.cloned.1.call-start = ((), (), s32[]{:S(2)}) async-start(), calls=%async_computation.4 | async-start | bytes 3342336 | tf_op jit(solution)/shard_map/reduce_scatter | solution.py:118
Sparse Core Ops, SparseCore 0:
  96.1 100.6 all-gather.1
  225.1 64.0 reduce-scatter.1
where the time goes:
time: 297 us; the launch traced here: 296 us
  waiting for transfers between devices  216 us (73%)
  local copies, waits for them, and re-layouts  32.5 us (11%)
  starting transfers between devices  15.5 us (5%)
  between operations  13.6 us (5%)
  matrix products  12.5 us (4%)
  other arithmetic  5.82 us (2%)
    all_gather x1, waiting for transfers between devices, body(): home_all = lax.all_gather(attended_rows, 'dp', axis=0, tiled=True)  99.9 us
    reduce_scatter x1, waiting for transfers between devices, body(): lax.psum_scatter(jnp.dot(picked, out_weight, preferred_element_type=jnp.f...  64.2 us
    all_to_all x1, waiting for transfers between devices, body(): lax.all_to_all(spread(cache_keys), 'tensor', split_axis=2, concat_axis=1,...  26.3 us
    all_to_all x1, waiting for transfers between devices, body(): lax.all_to_all(spread(cache_values), 'tensor', split_axis=2, concat_axis=...  25.4 us
    gather x1, local copies, waits for them, and re-layouts, body(): picked = jnp.take(home_all, request * DRAFT + within, axis=0)  20.4 us
    all_to_all x1, starting transfers between devices, body(): lax.all_to_all(spread(cache_keys), 'tensor', split_axis=2, concat_axis=1,...  10.4 us
    dot_general x1, matrix products, body(): jnp.dot(picked, out_weight, preferred_element_type=jnp.float32)  7.65 us
  transfers between devices with their start and end apart: 4, of which 4 were waited for; matrix products, arithmetic and copies ran while one was open for 1% of the time, Pallas kernels for 0%

commit v1 on v0

--- a/solution.py
+++ b/solution.py
@@ -91,7 +91,15 @@
         )
 
     full_keys, full_values = (
-        lax.all_to_all(spread(cache_keys), "tensor", split_axis=2, concat_axis=1, tiled=True),
+        jnp.concatenate(
+            lax.all_to_all(
+                jnp.stack(jnp.split(spread(cache_keys), lax.axis_size("tensor"), axis=2)),
+                "tensor",
+                0,
+                0,
+            ),
+            axis=1,
+        ),
         lax.all_to_all(spread(cache_values), "tensor", split_axis=2, concat_axis=1, tiled=True),
     )
     kv_first = my_rank * local_heads // group_heads

time: 297 us -> 294 us (0.990)
  the two profiles are of different devices: /device:TPU:8 before, /device:TPU:18 now
where the time goes in v1:
time: 294 us; the launch traced here: 293 us
  waiting for transfers between devices  212 us (72%)
  local copies, waits for them, and re-layouts  33.6 us (11%)
  starting transfers between devices  15.4 us (5%)
  between operations  13.7 us (5%)
  matrix products  12.5 us (4%)
  other arithmetic  5.59 us (2%)
    all_gather x1, waiting for transfers between devices, body(): home_all = lax.all_gather(attended_rows, 'dp', axis=0, tiled=True)  99.2 us
    reduce_scatter x1, waiting for transfers between devices, body(): lax.psum_scatter(jnp.dot(picked, out_weight, preferred_element_type=jnp.f...  64.8 us
    all_to_all x1, waiting for transfers between devices, body(): lax.all_to_all(spread(cache_values), 'tensor', split_axis=2, concat_axis=...  24.7 us
    all_to_all x1, waiting for transfers between devices, body(): lax.all_to_all(jnp.stack(jnp.split(spread(cache_keys), lax.axis_size('ten...  23.5 us
    gather x1, local copies, waits for them, and re-layouts, body(): picked = jnp.take(home_all, request * DRAFT + within, axis=0)  20.4 us
    all_to_all x1, starting transfers between devices, body(): lax.all_to_all(spread(cache_values), 'tensor', split_axis=2, concat_axis=...  10.4 us
    dot_general x1, matrix products, body(): jnp.dot(picked, out_weight, preferred_element_type=jnp.float32)  7.67 us
  transfers between devices with their start and end apart: 4, of which 4 were waited for; matrix products, arithmetic and copies ran while one was open for 1% of the time, Pallas kernels for 0%

profile of v1, /device:TPU:18, one launch (start us, length us, event | category | flops | bytes accessed | tf_op | source)
XLA Modules:
  0.0 293.3 jit_solution(9980169149079549998)
XLA Ops:
  6.5 1.3 copy_bitcast_fusion.4
  7.8 1.2 broadcast_in_dim.101
  9.0 10.4 %all-to-all-start = ((bf16[2,128,16,128]{3,1,0,2:T(8,128)(2,1)}), bf16[2,128,16,128]{3,1,0,2:T(8,128)(2,1)S(1)}, u32[]{:S(2)}, u32[]{:S(2)}) async-start(bf16[2,128,16,128]{3,1,0,2:T(8,128)(2,1)} %bitcast.20), calls=%async_computation | async-start | bytes 2097152 | tf_op jit(solution)/shard_map/all_to_all | solution.py:103
  20.3 1.0 copy-done.1
  21.3 24.7 %all-to-all-done = bf16[2,128,16,128]{3,1,0,2:T(8,128)(2,1)S(1)} async-done(((bf16[2,128,16,128]{3,1,0,2:T(8,128)(2,1)}), bf16[2,128,16,128]{3,1,0,2:T(8,128)(2,1)S(1)}, u32[]{:S(2)}, u32[]{:S(2)}) %all-to-all-start) | async-done | bytes 1048608 | tf_op jit(solution)/shard_map/all_to_all | solution.py:103
  46.0 4.9 %all-to-all-start.1 = ((bf16[16,2,128,1,128]{4,2,1,3,0:T(8,128)(2,1)}), bf16[16,2,128,1,128]{4,2,1,3,0:T(8,128)(2,1)S(1)}, u32[]{:S(2)}, u32[]{:S(2)}) async-start(bf16[16,2,128,1,128]{4,2,1,3,0:T(8,128)(2,1)} %copy-done.1), calls=%async_computation.1 | async-start | bytes 2097152 | tf_op jit(solution)/shard_map/all_to_all | solution.py:95
  51.0 1.0 copy.79
  52.1 0.8 constant_dynamic-slice_fusion.1
  52.9 1.0 copy.66
  53.9 23.5 %all-to-all-done.1 = bf16[16,2,128,1,128]{4,2,1,3,0:T(8,128)(2,1)S(1)} async-done(((bf16[16,2,128,1,128]{4,2,1,3,0:T(8,128)(2,1)}), bf16[16,2,128,1,128]{4,2,1,3,0:T(8,128)(2,1)S(1)}, u32[]{:S(2)}, u32[]{:S(2)}) %all-to-all-start.1) | async-done | bytes 1048608 | tf_op jit(solution)/shard_map/all_to_all | solution.py:95
  77.5 14.1 %while.10 = (s32[]{:T(128)}, bf16[2,64,1,8,128]{4,3,1,0,2:T(8,128)(2,1)}, s32[2]{0:T(128)S(1)}, bf16[2,2048,1,128]{3,1,2,0:T(8,128)(2,1)}, s32[2]{0:T(128)S(1)},...) while((s32[]{:T(128)}, ...), condition=%wide.region_8.9_spmd, body=%wide.region_3.8_spmd.sunk | while | flops 566699072 | bytes 21984120 | solution.py:114
  77.5 0.7 dynamic_slice.73
  78.2 0.6 iota_compare_fusion.6
  78.8 0.7 dynamic_slice.72
  79.5 0.6 iota_compare_fusion.5
  80.5 0.9 bitcast_reduce_fusion.2
  81.5 1.0 fusion.87
  82.4 1.1 fusion.89
  83.9 0.7 copy-done.5
  84.6 0.6 dynamic_slice.73
  85.2 0.6 iota_compare_fusion.6
  85.9 0.7 dynamic_slice.72
  86.5 0.6 iota_compare_fusion.5
  87.5 0.9 bitcast_reduce_fusion.2
  88.5 1.0 fusion.87
  89.5 1.1 fusion.89
  90.9 0.7 copy-done.5
  91.6 1.7 copy.92
  94.3 99.2 %all-gather.2.cloned.1.call-done = bf16[4096,1024]{1,0:T(8,128)(2,1)} async-done(((bf16[128,1024]{1,0:T(8,128)(2,1)}), bf16[4096,1024]{1,0:T(8,128)(2,1)}) %all-gather.2.cloned.1.call-update) | async-done | bytes 8388624 | tf_op jit(solution)/shard_map/all_gather | solution.py:121
  193.5 20.4 %gather_fusion = bf16[3072,1024]{1,0:T(8,128)(2,1)} fusion(bf16[4096,1024]{1,0:T(8,128)(2,1)} %all-gather.2.cloned.1.call-done, s32[3072]{0:T(1024)S(1)} %broadcast_clamp_fusion), kind=kCustom, calls=%fused_computation | custom fusion | bytes 12595200 | tf_op jit(solution)/shard_map/jit(_take)/gather | solution.py:124
  213.9 7.7 %fusion.34 = bf16[3072,512]{1,0:T(8,128)(2,1)} fusion(bf16[1024,512]{1,0:T(8,128)(2,1)S(1)} %copy-done, bf16[3072,1024]{1,0:T(8,128)(2,1)} %gather_fusion, pred[3072]{0:T(1024)(128)(4,1)S(1)} %compare_and_fusion.1, pred[3072]{0:T(1024)(128)(4,1)S(1)} %fusion.66), kind=kOutput, calls=%fused_computation.49 | convolution fusion | flops 3229089792 | bytes 10491904 | tf_op jit(solution)/shard_map/dot_general | solution.py:127
  221.6 64.8 %reduce-scatter.2.cloned.1.call-done = bf16[192,512]{1,0:T(8,128)(2,1)} async-done(((bf16[3072,512]{1,0:T(8,128)(2,1)}), bf16[192,512]{1,0:T(8,128)(2,1)}) %reduce-scatter.2.cloned.1.call-update) | async-done | bytes 196624 | tf_op jit(solution)/shard_map/reduce_scatter | solution.py:126
  (72 shorter events, 3.4 us)
Async XLA Ops:
  6.5 207.4 %copy-start = (bf16[1024,512]{1,0:T(8,128)(2,1)S(1)}, bf16[1024,512]{1,0:T(8,128)(2,1)}, u32[]{:S(2)}) copy-start(bf16[1024,512]{1,0:T(8,128)(2,1)} %param.17) | copy-start | bytes 3145732
  6.5 12.9 %copy-start.3 = (bf16[2,128,1024]{2,1,0:T(8,128)(2,1)S(1)}, bf16[2,128,1024]{2,1,0:T(8,128)(2,1)}, u32[]{:S(2)}) copy-start(bf16[2,128,1024]{2,1,0:T(8,128)(2,1)} %param.15) | copy-start | bytes 1572868
  9.0 36.9 %all-to-all-start = ((bf16[2,128,16,128]{3,1,0,2:T(8,128)(2,1)}), bf16[2,128,16,128]{3,1,0,2:T(8,128)(2,1)S(1)}, u32[]{:S(2)}, u32[]{:S(2)}) async-start(bf16[2,128,16,128]{3,1,0,2:T(8,128)(2,1)} %bitcast.20), calls=%async_computation | async-start | bytes 2097152 | tf_op jit(solution)/shard_map/all_to_all | solution.py:103
  19.5 32.5 %copy-start.9 = (s32[64]{0:T(128)S(1)}, s32[64]{0:T(128)}, u32[]{:S(2)}) copy-start(s32[64]{0:T(128)} %param.19) | copy-start | bytes 772
  20.0 57.5 %copy-start.8 = (s32[2]{0:T(128)S(1)}, s32[2]{0:T(128)}, u32[]{:S(2)}) copy-start(s32[2]{0:T(128)} %param.18) | copy-start | bytes 28
  20.2 1.0 copy-start.1
  46.0 31.4 %all-to-all-start.1 = ((bf16[16,2,128,1,128]{4,2,1,3,0:T(8,128)(2,1)}), bf16[16,2,128,1,128]{4,2,1,3,0:T(8,128)(2,1)S(1)}, u32[]{:S(2)}, u32[]{:S(2)}) async-start(bf16[16,2,128,1,128]{4,2,1,3,0:T(8,128)(2,1)} %copy-done.1), calls=%async_computation.1 | async-start | bytes 2097152 | tf_op jit(solution)/shard_map/all_to_all | solution.py:95
  50.9 142.6 %all-gather.2.cloned.1.call-start = ((), (), s32[]{:S(2)}) async-start(), calls=%async_computation.3 | async-start | bytes 8650752 | tf_op jit(solution)/shard_map/all_gather | solution.py:121
  77.5 15.9 %copy-start.6 = (s32[64]{0:T(128)S(1)}, s32[64]{0:T(128)}, u32[]{:S(2)}) copy-start(s32[64]{0:T(128)} %param.21) | copy-start | bytes 772
  77.5 15.9 %copy-start.7 = (s32[64]{0:T(128)S(1)}, s32[64]{0:T(128)}, u32[]{:S(2)}) copy-start(s32[64]{0:T(128)} %param.20) | copy-start | bytes 772
  80.5 1.9 copy-start.2
  82.4 1.3 copy-start.4
  83.9 0.7 copy-start.5
  87.5 1.9 copy-start.2
  89.4 1.3 copy-start.4
  90.9 0.7 copy-start.5
  93.4 193.1 %reduce-scatter.2.cloned.1.call-start = ((), (), s32[]{:S(2)}) async-start(), calls=%async_computation.4 | async-start | bytes 3342336 | tf_op jit(solution)/shard_map/reduce_scatter | solution.py:126
Sparse Core Ops, SparseCore 0:
  93.5 99.9 all-gather.1
  221.7 64.6 reduce-scatter.1
